TPU v7x, 256 devices: a whole 4x4x8 slice. The times are simulated.
256 devices in a mesh: dp: 16 (over z, core), feat: 16 (over x, y).
Axes of the slice: x: 4, y: 4, z: 8, core: 2. Of those that a mesh axis runs over, the one named last changes fastest.
Arguments:
- points: bfloat16 [4096, 256], P('dp'), may hold values from -6 to 6
- freqs: bfloat16 [256, 8192], P(None, 'feat'), may hold values from -0.375 to 0.375
- phase: float32 [8192], P('feat'), may hold values from -3.140625 to 3.140625
- ridge: float32 [8192], P('feat'), may hold values from 0.05 to 0.5
- targets: bfloat16 [8, 4096], P(None, 'dp'), may hold values from -6 to 6
Outputs:
- gram: float32 [8192, 8192], P('feat', 'dp')
- projected: float32 [8, 8192], P(None, 'feat')
- factors: float32 [8192, 1024], P('feat')
All inputs are finite; a program needn't handle non-finite values.
Results may differ from a plain program's by a relative error of at most 0.003.
Values may be sent and summed in bfloat16 or wider, within the bound.
A program may use at most 128 MiB of HBM per device.

v0:
```python
import math
import jax
import jax.numpy as jnp
from jax import lax
from jax.sharding import PartitionSpec as P

FB = 1024


def features(rows, freq_cols, phase_cols, scale):
    angle = jnp.dot(rows, freq_cols, preferred_element_type=jnp.float32) + phase_cols
    return (scale * jnp.cos(angle)).astype(jnp.bfloat16)


def cross(left, right):
    return lax.dot_general(
        left, right, (((0,), (0,)), ((), ())), preferred_element_type=jnp.float32
    )


def with_ridge(tile, ridge, row_start, col_start):
    rows_here = row_start + lax.broadcasted_iota(jnp.int32, tile.shape, 0)
    cols_here = col_start + lax.broadcasted_iota(jnp.int32, tile.shape, 1)
    return tile + jnp.where(rows_here == cols_here, ridge[:, None], 0.0)


def shards(points, freqs, phase, ridge, targets):
    data_count = lax.axis_size("dp")
    feat_count = lax.axis_size("feat")
    feat_index = lax.axis_index("feat")
    data_index = lax.axis_index("dp")
    local_width = freqs.shape[1]
    total_width = local_width * feat_count
    tile_width = total_width // data_count
    window = max(local_width, FB)
    window_start = feat_index * local_width // window * window
    row_start = feat_index * local_width
    col_start = data_index * tile_width
    scale = math.sqrt(2.0 / (points.shape[0] * data_count))
    points_all, targets_all = (
        lax.all_gather(points, "dp", axis=0, tiled=True),
        lax.all_gather(targets, "dp", axis=1, tiled=True),
    )
    freqs_wide, phase_all, ridge_all = (
        lax.all_gather(freqs.astype(jnp.float32), "feat", axis=1, tiled=True),
        lax.all_gather(phase, "feat", axis=0, tiled=True),
        lax.all_gather(ridge, "feat", axis=0, tiled=True),
    )
    freqs_all = freqs_wide.astype(jnp.bfloat16)
    row_phi = features(points_all, freqs, phase, scale)
    col_phi = features(
        points_all,
        lax.dynamic_slice_in_dim(freqs_all, col_start, tile_width, 1),
        lax.dynamic_slice_in_dim(phase_all, col_start, tile_width, 0),
        scale,
    )
    gram_tile = cross(row_phi, col_phi)
    window_phi = features(
        points_all,
        lax.dynamic_slice_in_dim(freqs_all, window_start, window, 1),
        lax.dynamic_slice_in_dim(phase_all, window_start, window, 0),
        scale,
    )
    projected = jnp.dot(targets_all, row_phi, preferred_element_type=jnp.float32)
    slab = cross(window_phi, window_phi)
    window_ridge = lax.dynamic_slice_in_dim(ridge_all, window_start, window, 0)
    slab = with_ridge(slab, window_ridge, window_start, window_start)
    gram_tile = with_ridge(gram_tile, ridge, row_start, col_start)
    block_count = window // FB
    stacked = jnp.stack([slab])
    factors_all = jnp.linalg.cholesky(stacked).reshape(window, FB)
    factor_rows = lax.dynamic_slice_in_dim(factors_all, row_start - window_start, local_width, 0)
    return (gram_tile, projected, factor_rows)


def solution(mesh):
    in_specs = (P("dp", None), P(None, "feat"), P("feat"), P("feat"), P(None, "dp"))
    out_specs = (P("feat", "dp"), P(None, "feat"), P("feat", None))
    return jax.shard_map(shards, mesh=mesh, in_specs=in_specs, out_specs=out_specs, check_vma=False)
```

profile of v0, /device:TPU:2, one launch (start us, length us, event | category | flops | bytes accessed | tf_op | source)
XLA Modules:
  0.0 462.8 jit_solution(10146078261034066194)
XLA Ops:
  8.7 23.4 %all-gather = f32[16,1,512]{2,1,0:T(1,128)S(1)} all-gather(f32[1,1,512]{2,1,0:T(1,128)} %bitcast.188), channel_id=1, replica_groups=mesh['dp'=16,'feat'=16] {'feat'}, dimensions={0}, use_global_device_ids=true | all-gather | bytes 34816 | tf_op jit(solution)/shard_map/all_gather | solution.py:46
  32.1 21.7 %all-gather.1 = f32[16,1,512]{2,1,0:T(1,128)S(1)} all-gather(f32[1,1,512]{2,1,0:T(1,128)} %bitcast.189), channel_id=1, replica_groups=mesh['dp'=16,'feat'=16] {'feat'}, dimensions={0}, use_global_device_ids=true | all-gather | bytes 34816 | tf_op jit(solution)/shard_map/all_gather | solution.py:47
  53.9 20.4 %all_gather.18 = bf16[8,4096]{1,0:T(8,128)(2,1)S(1)} all-gather(bf16[8,256]{1,0:T(8,128)(2,1)} %param.9), channel_id=1, replica_groups=mesh['dp'=16,'feat'=16] {'dp'}, dimensions={1}, use_global_device_ids=true | all-gather | bytes 69632 | tf_op jit(solution)/shard_map/all_gather | solution.py:42
  74.3 29.4 %multiply_convert_fusion.2 = bf16[4096,512]{1,0:T(8,128)(2,1)S(1)} fusion(bf16[4096,256]{1,0:T(8,128)(2,1)} %all-gather.5.cloned.1.call-done, bf16[256,512]{1,0:T(8,128)(2,1)} %param.6, f32[512]{0:T(512)} %param.7), kind=kOutput, calls=%fused_computation.2 | convolution fusion | flops 1080033280 | bytes 6555648 | tf_op jit(solution)/shard_map/dot_general | solution.py:11
  106.9 7.7 %all-gather.7.cloned.1.call-done = bf16[256,8192]{1,0:T(8,128)(2,1)} async-done(((bf16[256,512]{1,0:T(8,128)(2,1)}), bf16[256,8192]{1,0:T(8,128)(2,1)}) %all-gather.7.cloned.1.call-update) | async-done | bytes 4194320 | tf_op jit(solution)/shard_map/all_gather | solution.py:45
  114.6 59.9 %multiply_convert_fusion.clone.6 = bf16[1024,4096]{1,0:T(8,128)(2,1)} fusion(bf16[4096,256]{1,0:T(8,128)(2,1)S(1)} %copy-done.6, f32[1024]{0:T(1024)S(1)} %dynamic_slice.23, bf16[256,8192]{1,0:T(8,128)(2,1)} %all-gather.7.cloned.1.call-done, s32[]{:T(128)S(6)} %select_n.32), kind=kOutput, calls=%fused_computation.clone.clone.clone.2 | convolution fusion | flops 2160066560 | bytes 11014148 | tf_op jit(solution)/shard_map/dot_general | solution.py:11
  174.5 26.7 %fusion = f32[1024,1024]{0,1:T(8,128)S(1)} fusion(bf16[1024,4096]{1,0:T(8,128)(2,1)} %multiply_convert_fusion.clone.6), kind=kOutput, calls=%fused_computation.3 | convolution fusion | flops 8589934592 | bytes 12582912 | tf_op jit(solution)/shard_map/dot_general | solution.py:16
  205.5 5.3 %copy.11 = f32[1,1024,1024]{2,1,0:T(8,128)} copy(f32[1,1024,1024]{1,2,0:T(8,128)} %fusion.2) | data formatting | bytes 8388608 | tf_op jit(solution)/shard_map/stack | solution.py:70
  217.0 11.7 %custom-call.67 = f32[1,128,128]{2,1,0:T(8,128)S(1)} custom-call(f32[1,128,128]{2,1,0:T(8,128)S(1)} %cholesky.585), custom_call_target="Cholesky" | custom-call | tf_op jit(solution)/shard_map/jit(cholesky)/cholesky | solution.py:71
  231.3 9.8 %custom-call.68 = f32[1,1,128,128]{2,3,1,0:T(8,128)S(1)} custom-call(f32[1,1,128,128]{3,2,1,0:T(8,128)S(1)} %get-tuple-element.24), custom_call_target="InvertDiagBlocksLowerTriangular" | custom-call | tf_op jit(solution)/shard_map/jit(cholesky)/cholesky | solution.py:71
  245.0 11.7 %custom-call.69 = f32[1,128,128]{2,1,0:T(8,128)S(1)} custom-call(f32[1,128,128]{2,1,0:T(8,128)S(1)} %cholesky.589), custom_call_target="Cholesky" | custom-call | tf_op jit(solution)/shard_map/jit(cholesky)/cholesky | solution.py:71
  257.4 10.2 %custom-call.70 = f32[1,1,128,128]{2,3,1,0:T(8,128)S(1)} custom-call(f32[1,1,128,128]{3,2,1,0:T(8,128)S(1)} %get-tuple-element.21), custom_call_target="InvertDiagBlocksLowerTriangular" | custom-call | tf_op jit(solution)/shard_map/jit(cholesky)/cholesky | solution.py:71
  271.0 11.7 %custom-call.71 = f32[1,128,128]{2,1,0:T(8,128)S(1)} custom-call(f32[1,128,128]{2,1,0:T(8,128)S(1)} %cholesky.594), custom_call_target="Cholesky" | custom-call | tf_op jit(solution)/shard_map/jit(cholesky)/cholesky | solution.py:71
  283.3 9.8 %custom-call.72 = f32[1,1,128,128]{2,3,1,0:T(8,128)S(1)} custom-call(f32[1,1,128,128]{3,2,1,0:T(8,128)S(1)} %get-tuple-element.18), custom_call_target="InvertDiagBlocksLowerTriangular" | custom-call | tf_op jit(solution)/shard_map/jit(cholesky)/cholesky | solution.py:71
  296.6 11.9 %custom-call.73 = f32[1,128,128]{2,1,0:T(8,128)S(1)} custom-call(f32[1,128,128]{2,1,0:T(8,128)S(1)} %cholesky.599), custom_call_target="Cholesky" | custom-call | tf_op jit(solution)/shard_map/jit(cholesky)/cholesky | solution.py:71
  309.2 9.8 %custom-call.74 = f32[1,1,128,128]{2,3,1,0:T(8,128)S(1)} custom-call(f32[1,1,128,128]{3,2,1,0:T(8,128)S(1)} %get-tuple-element.15), custom_call_target="InvertDiagBlocksLowerTriangular" | custom-call | tf_op jit(solution)/shard_map/jit(cholesky)/cholesky | solution.py:71
  322.4 11.7 %custom-call.75 = f32[1,128,128]{2,1,0:T(8,128)S(1)} custom-call(f32[1,128,128]{2,1,0:T(8,128)S(1)} %cholesky.604), custom_call_target="Cholesky" | custom-call | tf_op jit(solution)/shard_map/jit(cholesky)/cholesky | solution.py:71
  334.8 9.8 %custom-call.76 = f32[1,1,128,128]{2,3,1,0:T(8,128)S(1)} custom-call(f32[1,1,128,128]{3,2,1,0:T(8,128)S(1)} %get-tuple-element.12), custom_call_target="InvertDiagBlocksLowerTriangular" | custom-call | tf_op jit(solution)/shard_map/jit(cholesky)/cholesky | solution.py:71
  348.1 11.7 %custom-call.77 = f32[1,128,128]{2,1,0:T(8,128)S(1)} custom-call(f32[1,128,128]{2,1,0:T(8,128)S(1)} %cholesky.609), custom_call_target="Cholesky" | custom-call | tf_op jit(solution)/shard_map/jit(cholesky)/cholesky | solution.py:71
  360.5 9.8 %custom-call.78 = f32[1,1,128,128]{2,3,1,0:T(8,128)S(1)} custom-call(f32[1,1,128,128]{3,2,1,0:T(8,128)S(1)} %get-tuple-element.9), custom_call_target="InvertDiagBlocksLowerTriangular" | custom-call | tf_op jit(solution)/shard_map/jit(cholesky)/cholesky | solution.py:71
  373.3 11.7 %custom-call.79 = f32[1,128,128]{2,1,0:T(8,128)S(1)} custom-call(f32[1,128,128]{2,1,0:T(8,128)S(1)} %cholesky.614), custom_call_target="Cholesky" | custom-call | tf_op jit(solution)/shard_map/jit(cholesky)/cholesky | solution.py:71
  385.6 10.2 %custom-call.80 = f32[1,1,128,128]{2,3,1,0:T(8,128)S(1)} custom-call(f32[1,1,128,128]{3,2,1,0:T(8,128)S(1)} %get-tuple-element.6), custom_call_target="InvertDiagBlocksLowerTriangular" | custom-call | tf_op jit(solution)/shard_map/jit(cholesky)/cholesky | solution.py:71
  398.4 11.7 %custom-call.81 = f32[1,128,128]{2,1,0:T(8,128)S(1)} custom-call(f32[1,128,128]{2,1,0:T(8,128)S(1)} %fusion.17), custom_call_target="Cholesky" | custom-call | tf_op jit(solution)/shard_map/jit(cholesky)/cholesky | solution.py:71
  420.5 30.2 %multiply_convert_fusion.1.clone.4 = bf16[512,4096]{1,0:T(8,128)(2,1)S(1)} fusion(bf16[4096,256]{1,0:T(8,128)(2,1)S(1)} %copy-done.6, f32[512]{0:T(512)S(1)} %dynamic_slice.21, bf16[256,8192]{1,0:T(8,128)(2,1)} %all-gather.7.cloned.1.call-done, s32[]{:T(128)S(6)} %select_n.29), kind=kOutput, calls=%fused_computation.1.clone.clone.clone.1 | convolution fusion | flops 1080033280 | bytes 6555652 | tf_op jit(solution)/shard_map/dot_general | solution.py:11
  (66 shorter events, 55.3 us)
Async XLA Ops:
  7.2 67.1 %all-gather.5.cloned.1.call-start = ((), (), s32[]{:S(2)}) async-start(), calls=%async_computation | async-start | bytes 2228224 | tf_op jit(solution)/shard_map/all_gather | solution.py:41
  7.9 106.7 %all-gather.7.cloned.1.call-start = ((), (), s32[]{:S(2)}) async-start(), calls=%async_computation.1 | async-start | bytes 4456448 | tf_op jit(solution)/shard_map/all_gather | solution.py:45
  103.7 2.0 copy-start.3
  105.7 9.0 %copy-start.6 = (bf16[4096,256]{1,0:T(8,128)(2,1)S(1)}, bf16[4096,256]{1,0:T(8,128)(2,1)}, u32[]{:S(2)}) copy-start(bf16[4096,256]{1,0:T(8,128)(2,1)} %all-gather.5.cloned.1.call-done) | copy-start | bytes 6291460
  201.2 1.9 copy-start.1
  215.1 1.9 copy-start.2
  420.5 30.2 %copy-start.4 = (bf16[4096,512]{1,0:T(8,128)(2,1)S(1)}, bf16[4096,512]{1,0:T(8,128)(2,1)}, u32[]{:S(2)}) copy-start(bf16[4096,512]{1,0:T(8,128)(2,1)} %copy-done.3) | copy-start | bytes 12582916
  420.5 30.2 %copy-start.5 = (f32[512]{0:T(512)S(1)}, f32[512]{0:T(512)}, u32[]{:S(2)}) copy-start(f32[512]{0:T(512)} %param.8) | copy-start | bytes 6148
  450.7 3.4 copy-start
Sparse Core Ops, SparseCore 0:
  9.8 42.3 all-gather.4
  54.6 59.9 all-gather.6
where the time goes:
time: 472 us; the launch traced here: 463 us
  other arithmetic  181 us (38%)
  matrix products  174 us (37%)
  blocking collectives  65.5 us (14%)
  between operations  19.6 us (4%)
  local copies, waits for them, and re-layouts  13.8 us (3%)
  waiting for transfers between devices  9.11 us (2%)
    another operation x30, other arithmetic, shards(): factors_all = jnp.linalg.cholesky(stacked).reshape(window, FB)  172 us
    dot_general x3, matrix products, features(): jnp.dot(rows, freq_cols, preferred_element_type=jnp.float32) + phase_cols  119 us
    dot_general x2, matrix products, cross(): lax.dot_general(left, right, (((0,), (0,)), ((), ())), preferred_element_...  30.1 us
    all_gather x1, blocking collectives, shards(): lax.all_gather(phase, 'feat', axis=0, tiled=True)  23.4 us
    another operation x14, matrix products, shards(): factors_all = jnp.linalg.cholesky(stacked).reshape(window, FB)  23.3 us
    all_gather x1, blocking collectives, shards(): lax.all_gather(ridge, 'feat', axis=0, tiled=True)  21.7 us
    all_gather x1, blocking collectives, shards(): lax.all_gather(targets, 'dp', axis=1, tiled=True)  20.4 us
  transfers between devices with their start and end apart: 2, of which 1 were waited for; matrix products, arithmetic and copies ran while one was open for 7% of the time, Pallas kernels for 0%

commit v1 on v0

--- a/solution.py
+++ b/solution.py
@@ -5,6 +5,11 @@
 from jax.sharding import PartitionSpec as P
 
 FB = 1024
+
+
+def gather_over(x, name, along):
+    outgoing = jnp.stack([x] * lax.axis_size(name))
+    return jnp.concatenate(lax.all_to_all(outgoing, name, 0, 0), axis=along)
 
 
 def features(rows, freq_cols, phase_cols, scale):
@@ -39,7 +44,7 @@
     scale = math.sqrt(2.0 / (points.shape[0] * data_count))
     points_all, targets_all = (
         lax.all_gather(points, "dp", axis=0, tiled=True),
-        lax.all_gather(targets, "dp", axis=1, tiled=True),
+        gather_over(targets, "dp", 1),
     )
     freqs_wide, phase_all, ridge_all = (
         lax.all_gather(freqs.astype(jnp.float32), "feat", axis=1, tiled=True),

time: 472 us -> 472 us (level)
  blocking collectives: 65.5 us -> 45.1 us
  waiting for transfers between devices: 9.11 us -> 18.3 us
  starting transfers between devices: 0.08 us -> 8.64 us
    all_gather x1 -> x0, blocking collectives: 20.4 us -> none  [shards(): lax.all_gather(targets, 'dp', axis=1, tiled=True)]
    all_gather x1, waiting for transfers between devices: 7.72 us -> 16.9 us  [shards(): lax.all_gather(freqs.astype(jnp.float32), 'feat', axis=1, tiled=True)]
    all_to_all x0 -> x1, starting transfers between devices: none -> 8.57 us  [gather_over(): return jnp.concatenate(lax.all_to_all(outgoing, name, 0, 0), axis=along)]
  transfers between devices with their start and end apart: 2 -> 3, of which waited for: 1 -> 1; matrix products, arithmetic and copies ran while one was open for 7% -> 8% of each run, Pallas kernels for 0% -> 0%
where the time goes in v1:
time: 472 us; the launch traced here: 463 us
  other arithmetic  181 us (38%)
  matrix products  177 us (38%)
  blocking collectives  45.1 us (10%)
  between operations  19.6 us (4%)
  waiting for transfers between devices  18.3 us (4%)
  local copies, waits for them, and re-layouts  13.1 us (3%)
  starting transfers between devices  8.64 us (2%)
    another operation x30, other arithmetic, shards(): factors_all = jnp.linalg.cholesky(stacked).reshape(window, FB)  172 us
    dot_general x3, matrix products, features(): jnp.dot(rows, freq_cols, preferred_element_type=jnp.float32) + phase_cols  120 us
    dot_general x2, matrix products, cross(): lax.dot_general(left, right, (((0,), (0,)), ((), ())), preferred_element_...  30.1 us
    all_gather x1, blocking collectives, shards(): lax.all_gather(phase, 'feat', axis=0, tiled=True)  23.4 us
    another operation x14, matrix products, shards(): factors_all = jnp.linalg.cholesky(stacked).reshape(window, FB)  23.3 us
    all_gather x1, blocking collectives, shards(): lax.all_gather(ridge, 'feat', axis=0, tiled=True)  21.7 us
    all_gather x1, waiting for transfers between devices, shards(): lax.all_gather(freqs.astype(jnp.float32), 'feat', axis=1, tiled=True)  16.9 us
  transfers between devices with their start and end apart: 3, of which 1 were waited for; matrix products, arithmetic and copies ran while one was open for 8% of the time, Pallas kernels for 0%

profile of v1, /device:TPU:2, one launch (start us, length us, event | category | flops | bytes accessed | tf_op | source)
XLA Modules:
  0.0 462.7 jit_solution(10866653751592048242)
XLA Ops:
  10.0 8.6 %all-to-all-start = ((bf16[16,8,256]{2,1,0:T(8,128)(2,1)}), bf16[16,8,256]{2,1,0:T(8,128)(2,1)S(1)}, u32[]{:S(2)}, u32[]{:S(2)}) async-start(bf16[16,8,256]{2,1,0:T(8,128)(2,1)} %stack.4), calls=%async_computation | async-start | bytes 131072 | tf_op jit(solution)/shard_map/all_to_all | solution.py:12
  18.6 23.4 %all-gather = f32[16,1,512]{2,1,0:T(1,128)S(1)} all-gather(f32[1,1,512]{2,1,0:T(1,128)} %bitcast.192), channel_id=1, replica_groups=mesh['dp'=16,'feat'=16] {'feat'}, dimensions={0}, use_global_device_ids=true | all-gather | bytes 34816 | tf_op jit(solution)/shard_map/all_gather | solution.py:51
  42.1 21.7 %all-gather.1 = f32[16,1,512]{2,1,0:T(1,128)S(1)} all-gather(f32[1,1,512]{2,1,0:T(1,128)} %bitcast.193), channel_id=1, replica_groups=mesh['dp'=16,'feat'=16] {'feat'}, dimensions={0}, use_global_device_ids=true | all-gather | bytes 34816 | tf_op jit(solution)/shard_map/all_gather | solution.py:52
  63.9 30.1 %multiply_convert_fusion.2 = bf16[4096,512]{1,0:T(8,128)(2,1)} fusion(bf16[4096,256]{1,0:T(8,128)(2,1)} %all-gather.5.cloned.1.call-done, bf16[256,512]{1,0:T(8,128)(2,1)} %param.6, f32[512]{0:T(512)} %param.7), kind=kOutput, calls=%fused_computation.2 | convolution fusion | flops 1080033280 | bytes 6555648 | tf_op jit(solution)/shard_map/dot_general | solution.py:16
  97.6 16.9 %all-gather.7.cloned.1.call-done = bf16[256,8192]{1,0:T(8,128)(2,1)} async-done(((bf16[256,512]{1,0:T(8,128)(2,1)}), bf16[256,8192]{1,0:T(8,128)(2,1)}) %all-gather.7.cloned.1.call-update) | async-done | bytes 4194320 | tf_op jit(solution)/shard_map/all_gather | solution.py:50
  114.5 59.9 %multiply_convert_fusion.clone.6 = bf16[1024,4096]{1,0:T(8,128)(2,1)} fusion(bf16[4096,256]{1,0:T(8,128)(2,1)S(1)} %copy-done.5, f32[1024]{0:T(1024)S(1)} %dynamic_slice.23, bf16[256,8192]{1,0:T(8,128)(2,1)} %all-gather.7.cloned.1.call-done, s32[]{:T(128)S(6)} %select_n.32), kind=kOutput, calls=%fused_computation.clone.clone.clone.2 | convolution fusion | flops 2160066560 | bytes 11014148 | tf_op jit(solution)/shard_map/dot_general | solution.py:16
  174.4 26.7 %fusion = f32[1024,1024]{0,1:T(8,128)S(1)} fusion(bf16[1024,4096]{1,0:T(8,128)(2,1)} %multiply_convert_fusion.clone.6), kind=kOutput, calls=%fused_computation.3 | convolution fusion | flops 8589934592 | bytes 12582912 | tf_op jit(solution)/shard_map/dot_general | solution.py:21
  205.4 5.3 %copy.11 = f32[1,1024,1024]{2,1,0:T(8,128)} copy(f32[1,1024,1024]{1,2,0:T(8,128)} %fusion.2) | data formatting | bytes 8388608 | tf_op jit(solution)/shard_map/stack | solution.py:75
  216.9 11.7 %custom-call.67 = f32[1,128,128]{2,1,0:T(8,128)S(1)} custom-call(f32[1,128,128]{2,1,0:T(8,128)S(1)} %cholesky.585), custom_call_target="Cholesky" | custom-call | tf_op jit(solution)/shard_map/jit(cholesky)/cholesky | solution.py:76
  231.2 9.8 %custom-call.68 = f32[1,1,128,128]{2,3,1,0:T(8,128)S(1)} custom-call(f32[1,1,128,128]{3,2,1,0:T(8,128)S(1)} %get-tuple-element.24), custom_call_target="InvertDiagBlocksLowerTriangular" | custom-call | tf_op jit(solution)/shard_map/jit(cholesky)/cholesky | solution.py:76
  244.9 11.7 %custom-call.69 = f32[1,128,128]{2,1,0:T(8,128)S(1)} custom-call(f32[1,128,128]{2,1,0:T(8,128)S(1)} %cholesky.589), custom_call_target="Cholesky" | custom-call | tf_op jit(solution)/shard_map/jit(cholesky)/cholesky | solution.py:76
  257.3 10.2 %custom-call.70 = f32[1,1,128,128]{2,3,1,0:T(8,128)S(1)} custom-call(f32[1,1,128,128]{3,2,1,0:T(8,128)S(1)} %get-tuple-element.21), custom_call_target="InvertDiagBlocksLowerTriangular" | custom-call | tf_op jit(solution)/shard_map/jit(cholesky)/cholesky | solution.py:76
  270.8 11.7 %custom-call.71 = f32[1,128,128]{2,1,0:T(8,128)S(1)} custom-call(f32[1,128,128]{2,1,0:T(8,128)S(1)} %cholesky.594), custom_call_target="Cholesky" | custom-call | tf_op jit(solution)/shard_map/jit(cholesky)/cholesky | solution.py:76
  283.2 9.8 %custom-call.72 = f32[1,1,128,128]{2,3,1,0:T(8,128)S(1)} custom-call(f32[1,1,128,128]{3,2,1,0:T(8,128)S(1)} %get-tuple-element.18), custom_call_target="InvertDiagBlocksLowerTriangular" | custom-call | tf_op jit(solution)/shard_map/jit(cholesky)/cholesky | solution.py:76
  296.5 11.9 %custom-call.73 = f32[1,128,128]{2,1,0:T(8,128)S(1)} custom-call(f32[1,128,128]{2,1,0:T(8,128)S(1)} %cholesky.599), custom_call_target="Cholesky" | custom-call | tf_op jit(solution)/shard_map/jit(cholesky)/cholesky | solution.py:76
  309.0 9.8 %custom-call.74 = f32[1,1,128,128]{2,3,1,0:T(8,128)S(1)} custom-call(f32[1,1,128,128]{3,2,1,0:T(8,128)S(1)} %get-tuple-element.15), custom_call_target="InvertDiagBlocksLowerTriangular" | custom-call | tf_op jit(solution)/shard_map/jit(cholesky)/cholesky | solution.py:76
  322.3 11.7 %custom-call.75 = f32[1,128,128]{2,1,0:T(8,128)S(1)} custom-call(f32[1,128,128]{2,1,0:T(8,128)S(1)} %cholesky.604), custom_call_target="Cholesky" | custom-call | tf_op jit(solution)/shard_map/jit(cholesky)/cholesky | solution.py:76
  334.7 9.8 %custom-call.76 = f32[1,1,128,128]{2,3,1,0:T(8,128)S(1)} custom-call(f32[1,1,128,128]{3,2,1,0:T(8,128)S(1)} %get-tuple-element.12), custom_call_target="InvertDiagBlocksLowerTriangular" | custom-call | tf_op jit(solution)/shard_map/jit(cholesky)/cholesky | solution.py:76
  348.0 11.7 %custom-call.77 = f32[1,128,128]{2,1,0:T(8,128)S(1)} custom-call(f32[1,128,128]{2,1,0:T(8,128)S(1)} %cholesky.609), custom_call_target="Cholesky" | custom-call | tf_op jit(solution)/shard_map/jit(cholesky)/cholesky | solution.py:76
  360.4 9.8 %custom-call.78 = f32[1,1,128,128]{2,3,1,0:T(8,128)S(1)} custom-call(f32[1,1,128,128]{3,2,1,0:T(8,128)S(1)} %get-tuple-element.9), custom_call_target="InvertDiagBlocksLowerTriangular" | custom-call | tf_op jit(solution)/shard_map/jit(cholesky)/cholesky | solution.py:76
  373.2 11.7 %custom-call.79 = f32[1,128,128]{2,1,0:T(8,128)S(1)} custom-call(f32[1,128,128]{2,1,0:T(8,128)S(1)} %cholesky.614), custom_call_target="Cholesky" | custom-call | tf_op jit(solution)/shard_map/jit(cholesky)/cholesky | solution.py:76
  385.5 10.2 %custom-call.80 = f32[1,1,128,128]{2,3,1,0:T(8,128)S(1)} custom-call(f32[1,1,128,128]{3,2,1,0:T(8,128)S(1)} %get-tuple-element.6), custom_call_target="InvertDiagBlocksLowerTriangular" | custom-call | tf_op jit(solution)/shard_map/jit(cholesky)/cholesky | solution.py:76
  398.3 11.7 %custom-call.81 = f32[1,128,128]{2,1,0:T(8,128)S(1)} custom-call(f32[1,128,128]{2,1,0:T(8,128)S(1)} %fusion.17), custom_call_target="Cholesky" | custom-call | tf_op jit(solution)/shard_map/jit(cholesky)/cholesky | solution.py:76
  420.4 30.2 %multiply_convert_fusion.1.clone.4 = bf16[512,4096]{1,0:T(8,128)(2,1)S(1)} fusion(bf16[4096,256]{1,0:T(8,128)(2,1)S(1)} %copy-done.5, f32[512]{0:T(512)S(1)} %dynamic_slice.21, bf16[256,8192]{1,0:T(8,128)(2,1)} %all-gather.7.cloned.1.call-done, s32[]{:T(128)S(6)} %select_n.29), kind=kOutput, calls=%fused_computation.1.clone.clone.clone.1 | convolution fusion | flops 1080033280 | bytes 6555652 | tf_op jit(solution)/shard_map/dot_general | solution.py:16
  (66 shorter events, 57.0 us)
Async XLA Ops:
  7.2 56.7 %all-gather.5.cloned.1.call-start = ((), (), s32[]{:S(2)}) async-start(), calls=%async_computation.1 | async-start | bytes 2228224 | tf_op jit(solution)/shard_map/all_gather | solution.py:46
  7.9 106.6 %all-gather.7.cloned.1.call-start = ((), (), s32[]{:S(2)}) async-start(), calls=%async_computation.2 | async-start | bytes 4456448 | tf_op jit(solution)/shard_map/all_gather | solution.py:50
  10.0 84.0 %all-to-all-start = ((bf16[16,8,256]{2,1,0:T(8,128)(2,1)}), bf16[16,8,256]{2,1,0:T(8,128)(2,1)S(1)}, u32[]{:S(2)}, u32[]{:S(2)}) async-start(bf16[16,8,256]{2,1,0:T(8,128)(2,1)} %stack.4), calls=%async_computation | async-start | bytes 131072 | tf_op jit(solution)/shard_map/all_to_all | solution.py:12
  94.0 20.5 %copy-start.5 = (bf16[4096,256]{1,0:T(8,128)(2,1)S(1)}, bf16[4096,256]{1,0:T(8,128)(2,1)}, u32[]{:S(2)}) copy-start(bf16[4096,256]{1,0:T(8,128)(2,1)} %all-gather.5.cloned.1.call-done) | copy-start | bytes 6291460
  201.1 1.9 copy-start.1
  215.0 1.9 copy-start.2
  420.4 30.2 %copy-start.3 = (bf16[4096,512]{1,0:T(8,128)(2,1)S(1)}, bf16[4096,512]{1,0:T(8,128)(2,1)}, u32[]{:S(2)}) copy-start(bf16[4096,512]{1,0:T(8,128)(2,1)} %multiply_convert_fusion.2) | copy-start | bytes 12582916
  420.4 30.2 %copy-start.4 = (f32[512]{0:T(512)S(1)}, f32[512]{0:T(512)}, u32[]{:S(2)}) copy-start(f32[512]{0:T(512)} %param.8) | copy-start | bytes 6148
  450.6 3.4 copy-start
Sparse Core Ops, SparseCore 0:
  9.8 42.3 all-gather.4
  54.6 59.8 all-gather.6
